TPU v7x, 256 devices: a whole 4x4x8 slice. The times are simulated.
256 devices in a mesh: ep: 128 (over z, x, y), half: 2 (over core).
Axes of the slice: x: 4, y: 4, z: 8, core: 2. Of those that a mesh axis runs over, the one named last changes fastest.
Arguments:
- tokens: bfloat16 [16384, 2048], P('ep', 'half'), may hold values from -6 to 6
- gate_weights: float32 [16384, 8], P('ep'), may hold values from 0.05 to 0.3
- expert_ids: int32 [16384, 8], P('ep'), may hold values from 0 to 127, all different within a row; in each aligned block of 128 rows (0 to 127, 128 to 255, ...) at most 10 rows name the same one
- w_gate: bfloat16 [128, 2048, 768], P('ep', None, 'half'), may hold values from -0.125 to 0.125
- w_up: bfloat16 [128, 2048, 768], P('ep', None, 'half'), may hold values from -0.125 to 0.125
- w_down: bfloat16 [128, 768, 2048], P('ep', 'half'), may hold values from -0.21875 to 0.21875
Outputs:
- mixed: bfloat16 [16384, 2048], P('ep', 'half')
Inputs may be any that keep to these rules, and one draw needn't show every extreme that they name: `expert_ids`: each row names 8 different experts. Within the rows of one device (aligned blocks of 128 rows) no expert is named by more than 10 rows, and in every draw some expert is named by exactly 10 rows of some block.
All inputs are finite; a program needn't handle non-finite values.
Results may differ from a plain program's by a relative error of at most 0.0085.
Values may be sent and summed in bfloat16 or wider, within the bound.
A program may use at most 64 MiB of HBM per device.

v0:
```python
import jax
import jax.numpy as jnp
from jax import lax
from jax.sharding import PartitionSpec as P


def cut_along(value, dim, size):
    lengths = value.shape
    blocks = value.reshape(*lengths[:dim], size, lengths[dim] // size, *lengths[dim + 1 :])
    return jnp.moveaxis(blocks, dim, 0)


def summed_on_arrival(value, axis, dim):
    size = lax.axis_size(axis)
    blocks = lax.all_to_all(cut_along(value, dim, size), axis, 0, 0, tiled=True)
    return jnp.sum(blocks.astype(jnp.float32), axis=0)


def local(tokens, gate_weights, expert_ids, w_gate, w_up, w_down):
    tok_dev, half_width = tokens.shape
    top = expert_ids.shape[1]
    local_experts = w_gate.shape[0]
    experts = local_experts * lax.axis_size("ep")
    capacity = min(tok_dev, max(2, 5 * tok_dev * top // (4 * experts)))
    flat_ids = expert_ids.reshape(-1)
    columns = jnp.arange(experts, dtype=jnp.int32)
    onehot = (flat_ids[:, None] == columns[None, :]).astype(jnp.int32)
    ranks = jnp.sum((jnp.cumsum(onehot, axis=0) - onehot) * onehot, axis=1)
    slot = flat_ids * capacity + ranks
    token_of_pair = jnp.arange(tok_dev * top, dtype=jnp.int32) // top
    token_table = jnp.zeros((experts * capacity,), jnp.int32).at[slot].set(token_of_pair)
    filled = (
        jnp.zeros((experts * capacity,), jnp.bfloat16)
        .at[slot]
        .set(jnp.ones((tok_dev * top,), jnp.bfloat16))
    )
    outgoing = (tokens[token_table] * filled[:, None]).reshape(experts, capacity, half_width)
    received = lax.all_to_all(outgoing, "ep", split_axis=0, concat_axis=0, tiled=True)
    count = received.shape[1]
    whole = lax.all_gather(received, "half", axis=2, tiled=True)
    width = whole.shape[2]
    grouped = whole.reshape(-1, local_experts, count, width)
    gate = jnp.einsum("secd,edf->secf", grouped, w_gate, preferred_element_type=jnp.float32)
    up = jnp.einsum("secd,edf->secf", grouped, w_up, preferred_element_type=jnp.float32)
    hidden = (jax.nn.silu(gate) * up).astype(jnp.bfloat16)
    partial_out = jnp.einsum("secf,efd->secd", hidden, w_down, preferred_element_type=jnp.float32)
    partial_out = partial_out.astype(jnp.bfloat16).reshape(experts, count, width)
    widened = lax.optimization_barrier(partial_out).astype(jnp.float32)
    summed = summed_on_arrival(widened.astype(jnp.bfloat16), "half", 2).astype(jnp.bfloat16)
    answer = lax.all_to_all(summed, "ep", split_axis=0, concat_axis=0, tiled=True)
    picked = answer.reshape(experts * capacity, -1)[slot].reshape(tok_dev, top, -1)
    slot_out = picked.astype(jnp.float32)
    mixed = jnp.einsum("tk,tkx->tx", gate_weights, slot_out)
    return mixed.astype(jnp.bfloat16)


def solution(mesh):
    placed = (
        P("ep", "half"),
        P("ep", None),
        P("ep", None),
        P("ep", None, "half"),
        P("ep", None, "half"),
        P("ep", "half", None),
    )
    return jax.shard_map(
        local, mesh=mesh, in_specs=placed, out_specs=P("ep", "half"), check_vma=False
    )
```

profile of v0, /device:TPU:8, one launch (start us, length us, event | category | flops | bytes accessed | tf_op | source)
XLA Modules:
  0.0 341.3 jit_solution(1037426813920486707)
XLA Ops:
  6.5 0.0 copy-start
  6.5 0.0 copy-start.1
  6.5 0.0 all-gather.2.cloned.1.call-start
  6.5 0.9 copy.24
  7.5 0.1 eq.29
  7.6 0.1 eq.25
  7.6 0.7 broadcast_multiply_fusion.1
  8.3 0.1 copy.26
  8.4 0.2 fusion.17
  8.7 0.1 copy.27
  8.8 0.1 copy.23
  9.0 0.1 mul.39
  9.1 0.4 fusion.16
  9.4 4.3 %scatter_custom_fusion = s32[1280]{0:T(1024)S(1)} fusion(s32[1024]{0:T(1024)S(1)} %bitcast.85, s32[1024]{0:T(1024)S(1)} %add_select_fusion, s32[]{:T(128)} %constant.29.clone.1), kind=kCustom, calls=%fused_computation.41 | custom fusion | bytes 5124 | tf_op jit(solution)/shard_map/scatter | solution.py:31
  13.8 0.0 copy-done.1
  13.8 5.1 %gather_fusion = bf16[1280,1024]{1,0:T(8,128)(2,1)} fusion(bf16[128,1024]{1,0:T(8,128)(2,1)S(1)} %copy-done.1, s32[2048]{0:T(1024)S(1)} %pad_clamp_fusion), kind=kCustom, calls=%fused_computation | custom fusion | bytes 5248000 | tf_op jit(solution)/shard_map/gather | solution.py:37
  18.9 5.9 %gather.9 = bf16[128,10,1024]{2,1,0:T(8,128)(2,1)} reshape(bf16[1280,1024]{1,0:T(8,128)(2,1)} %gather_fusion) | data formatting | bytes 5242880 | tf_op jit(solution)/shard_map/gather | solution.py:37
  24.8 7.6 %scatter_custom_fusion.1 = bf16[1280]{0:T(1024)(128)(2,1)S(1)} fusion(s32[1024]{0:T(1024)S(1)} %bitcast.86, bf16[1024]{0:T(1024)(128)(2,1)S(1)} %broadcast.65, bf16[]{:T(256)} %constant.37.clone.1), kind=kCustom, calls=%fused_computation.45 | custom fusion | bytes 2562 | tf_op jit(solution)/shard_map/scatter | solution.py:35
  32.4 0.2 mul.41
  32.6 2.5 broadcast_multiply_fusion
  35.1 110.6 %all_to_all.15 = bf16[128,10,1024]{2,1,0:T(8,128)(2,1)S(1)} all-to-all(bf16[128,10,1024]{2,1,0:T(8,128)(2,1)S(1)} %broadcast_multiply_fusion), channel_id=1, replica_groups=mesh['ep'=128,'half'=2] {'ep'}, dimensions={0} | all-to-all | bytes 5242880 | tf_op jit(solution)/shard_map/all_to_all | solution.py:38
  145.8 2.9 copy.28
  148.7 0.0 all-gather.2.cloned.1.call-update
  148.7 17.5 %all-gather.2.cloned.1.call-done = bf16[128,10,2048]{2,0,1:T(8,128)(2,1)} async-done(((bf16[128,10,1024]{2,0,1:T(8,128)(2,1)}), bf16[128,10,2048]{2,0,1:T(8,128)(2,1)}) %all-gather.2.cloned.1.call-update) | async-done | bytes 5242896 | tf_op jit(solution)/shard_map/all_gather | solution.py:40
  166.2 7.1 %fusion.8 = f32[128,10,384]{2,0,1:T(8,128)} fusion(bf16[128,10,2048]{2,0,1:T(8,128)(2,1)} %all-gather.2.cloned.1.call-done, bf16[1,2048,384]{2,1,0:T(8,128)(2,1)} %param.9), kind=kOutput, calls=%fused_computation.18 | convolution fusion | flops 2013265920 | bytes 8781824 | tf_op jit(solution)/shard_map/secd,edf->secf/dot_general | solution.py:43
  173.3 0.0 copy-done
  173.3 9.8 %convolution_convert_fusion = bf16[128,10,2048]{2,0,1:T(8,128)(2,1)} fusion(bf16[1,384,2048]{2,1,0:T(8,128)(2,1)S(1)} %copy-done, bf16[128,10,2048]{2,0,1:T(8,128)(2,1)} %all-gather.2.cloned.1.call-done, bf16[1,2048,384]{2,1,0:T(8,128)(2,1)} %param.10, f32[128,10,384]{2,0,1:T(8,128)} %fusion.8), kind=kOutput, calls=%fused_computation.5 | convolution fusion | flops 4032102400 | bytes 15597568 | tf_op jit(solution)/shard_map/secf,efd->secd/dot_general | solution.py:46
  183.1 3.3 copy.38
  186.4 9.1 %all_to_all.16 = bf16[2,128,10,1024]{3,1,2,0:T(8,128)(2,1)} all-to-all(bf16[2,128,10,1024]{3,1,2,0:T(8,128)(2,1)S(1)} %bitcast.82), channel_id=1, replica_groups=mesh['ep'=128,'half'=2] {'half'}, dimensions={0} | all-to-all | bytes 10485760 | tf_op jit(solution)/shard_map/all_to_all | solution.py:15
  195.5 6.2 %reduce_sum.25 = bf16[128,10,1024]{2,0,1:T(8,128)(2,1)} reduce(bf16[2,128,10,1024]{3,1,2,0:T(8,128)(2,1)} %all_to_all.16, bf16[]{:T(256)} %constant.37.clone.1), dimensions={0}, to_apply=%region_5.6 | reduce | flops 1310720 | bytes 7864322 | tf_op jit(solution)/shard_map/reduce_sum | solution.py:16
  201.8 5.3 %copy.31 = bf16[128,10,1024]{2,1,0:T(8,128)(2,1)} copy(bf16[128,10,1024]{2,0,1:T(8,128)(2,1)} %reduce_sum.25) | data formatting | bytes 5242880 | tf_op jit(solution)/shard_map/reduce_sum | solution.py:16
  207.1 0.0 copy-start.2
  207.1 14.3 %all-to-all-start.2 = ((bf16[128,10,1024]{2,1,0:T(8,128)(2,1)}), bf16[128,10,1024]{2,1,0:T(8,128)(2,1)}, u32[]{:S(2)}, u32[]{:S(2)}) async-start(bf16[128,10,1024]{2,1,0:T(8,128)(2,1)} %copy.31), calls=%async_computation.2 | async-start | bytes 8388608 | tf_op jit(solution)/shard_map/all_to_all | solution.py:50
  221.5 0.0 copy-done.2
  221.5 0.1 copy.32
  221.6 95.5 %all-to-all-done.2 = bf16[128,10,1024]{2,1,0:T(8,128)(2,1)} async-done(((bf16[128,10,1024]{2,1,0:T(8,128)(2,1)}), bf16[128,10,1024]{2,1,0:T(8,128)(2,1)}, u32[]{:S(2)}, u32[]{:S(2)}) %all-to-all-start.2) | async-done | bytes 2621472 | tf_op jit(solution)/shard_map/all_to_all | solution.py:50
  317.1 6.1 %reshape.91 = bf16[1280,1024]{1,0:T(8,128)(2,1)} reshape(bf16[128,10,1024]{2,1,0:T(8,128)(2,1)} %all-to-all-done.2) | data formatting | bytes 5242880 | tf_op jit(solution)/shard_map/reshape | solution.py:51
  323.3 8.1 %gather_fusion.1 = bf16[1024,1024]{1,0:T(8,128)(2,1)} fusion(bf16[1280,1024]{1,0:T(8,128)(2,1)} %reshape.91, s32[1024]{0:T(1024)S(1)} %broadcast_clamp_fusion), kind=kCustom, calls=%fused_computation.1 | custom fusion | bytes 4198400 | tf_op jit(solution)/shard_map/gather | solution.py:51
  331.4 2.3 fusion
  333.7 0.8 copy.39
  (10 shorter events, 0.1 us)
Async XLA Ops:
  6.5 166.8 %copy-start = (bf16[1,384,2048]{2,1,0:T(8,128)(2,1)S(1)}, bf16[1,384,2048]{2,1,0:T(8,128)(2,1)}, u32[]{:S(2)}) copy-start(bf16[1,384,2048]{2,1,0:T(8,128)(2,1)} %param.11) | copy-start | bytes 4718596
  6.5 7.2 %copy-start.1 = (bf16[128,1024]{1,0:T(8,128)(2,1)S(1)}, bf16[128,1024]{1,0:T(8,128)(2,1)}, u32[]{:S(2)}) copy-start(bf16[128,1024]{1,0:T(8,128)(2,1)} %param.6) | copy-start | bytes 786436
  6.5 159.7 %all-gather.2.cloned.1.call-start = ((), (), s32[]{:S(2)}) async-start(), calls=%async_computation.3 | async-start | bytes 7864320 | tf_op jit(solution)/shard_map/all_gather | solution.py:40
  207.1 14.4 %copy-start.2 = (f32[128,8]{0,1:T(8,128)S(1)}, f32[128,8]{0,1:T(8,128)}, u32[]{:S(2)}) copy-start(f32[128,8]{0,1:T(8,128)} %param.7) | copy-start | bytes 12292
  207.1 110.0 %all-to-all-start.2 = ((bf16[128,10,1024]{2,1,0:T(8,128)(2,1)}), bf16[128,10,1024]{2,1,0:T(8,128)(2,1)}, u32[]{:S(2)}, u32[]{:S(2)}) async-start(bf16[128,10,1024]{2,1,0:T(8,128)(2,1)} %copy.31), calls=%async_computation.2 | async-start | bytes 8388608 | tf_op jit(solution)/shard_map/all_to_all | solution.py:50
Sparse Core Ops, SparseCore 0:
  148.9 17.2 all-gather.1
where the time goes:
time: 342 us; the launch traced here: 341 us
  blocking collectives  120 us (35%)
  waiting for transfers between devices  113 us (33%)
  local copies, waits for them, and re-layouts  51.4 us (15%)
  matrix products  19.2 us (6%)
  starting transfers between devices  14.3 us (4%)
  between operations  13.5 us (4%)
  other arithmetic  10.1 us (3%)
    all_to_all x1, blocking collectives, local(): lax.all_to_all(outgoing, 'ep', split_axis=0, concat_axis=0, tiled=True)  111 us
    all_to_all x1, waiting for transfers between devices, local(): lax.all_to_all(summed, 'ep', split_axis=0, concat_axis=0, tiled=True)  95.5 us
    all_gather x1, waiting for transfers between devices, local(): whole = lax.all_gather(received, 'half', axis=2, tiled=True)  17.5 us
    all_to_all x1, starting transfers between devices, local(): lax.all_to_all(summed, 'ep', split_axis=0, concat_axis=0, tiled=True)  14.3 us
    gather x2, local copies, waits for them, and re-layouts, local(): tokens[token_table] * filled[:, None]  11 us
    dot_general x1, matrix products, local(): jnp.einsum('secf,efd->secd', hidden, w_down, preferred_element_type=jnp.f...  9.81 us
    all_to_all x1, blocking collectives, summed_on_arrival(): blocks = lax.all_to_all(cut_along(value, dim, size), axis, 0, 0, tiled=True)  9.08 us
    gather x1, local copies, waits for them, and re-layouts, local(): answer.reshape(experts * capacity, -1)[slot].reshape(tok_dev, top, -1)  8.11 us
  transfers between devices with their start and end apart: 2, of which 2 were waited for; matrix products, arithmetic and copies ran while one was open for 0% of the time, Pallas kernels for 0%

commit v1 on v0

v1 whole, which is shorter than its diff:
```python
import functools

import jax
import jax.numpy as jnp
from jax import lax
from jax.experimental import pallas as pl
from jax.experimental.pallas import tpu as pltpu
from jax.sharding import PartitionSpec as P

NZ, NX, NY = 8, 4, 4
PLANE = NX * NY
CAP = 10
SLOTS = NZ * CAP
BF = jnp.bfloat16
F32 = jnp.float32
CHUNKS = ((0, 256), (256, 256), (512, 256), (768, 256))


def kernel(
    tokens, meta, w_gate, w_up, w_down, out,
    x_all, meta_all, slot_of, weight_of, pack, comb, packed, rows, w_gu, w_dn, acc, hidden,
    y_out, y_in, part, red_out, red_in,
    meta_s, meta_r, zg_s, zg_r, d_s, d_r, b_s, b_r, zr_s, zr_r, wl, ws, wr,
):
    ep = lax.axis_index("ep")
    h = lax.axis_index("half")
    z = lax.div(ep, PLANE)
    xy = lax.rem(ep, PLANE)
    x = lax.div(xy, NY)
    y = lax.rem(xy, NY)
    up = lax.rem(z + 1, NZ) * PLANE + xy
    down = lax.rem(z + NZ - 1, NZ) * PLANE + xy
    tok, half_width = tokens.shape
    ff_half = w_gate.shape[2]
    ff = 2 * ff_half
    nrow = (PLANE // 2) * SLOTS

    def remote(src, dst, s, r, to_ep, to_h):
        return pltpu.make_async_remote_copy(
            src_ref=src, dst_ref=dst, send_sem=s, recv_sem=r,
            device_id={"ep": to_ep, "half": to_h}, device_id_type=pl.DeviceIdType.MESH,
        )

    barrier = pltpu.get_barrier_semaphore()

    def greet_plane(i, _):
        other = lax.rem(xy * 2 + h + i, 2 * PLANE)
        pl.semaphore_signal(
            barrier, 1,
            device_id={"ep": z * PLANE + lax.div(other, 2), "half": lax.rem(other, 2)},
            device_id_type=pl.DeviceIdType.MESH,
        )
        return 0

    def greet_z(i, _):
        pl.semaphore_signal(
            barrier, 1,
            device_id={"ep": lax.rem(z + i, NZ) * PLANE + xy, "half": h},
            device_id_type=pl.DeviceIdType.MESH,
        )
        return 0

    lax.fori_loop(1, NZ, greet_z, 0)
    lax.fori_loop(1, 2 * PLANE, greet_plane, 0)
    pl.semaphore_wait(barrier, NZ - 1 + 2 * PLANE - 1)

    def meta_copy(i):
        return remote(
            meta, meta_all.at[i], meta_s.at[i], meta_r.at[i],
            lax.rem(z + i, NZ) * PLANE + xy, h,
        )

    def up_len(c):
        return 4 if c % 2 == 0 else 3

    def cols(c):
        return pl.ds(*CHUNKS[c])

    def gather_copy(c, pos, upward, own=False):
        src_pos = pos - 1 if upward else pos + 1
        src = tokens.at[:, cols(c)] if own else x_all.at[src_pos, :, cols(c)]
        return remote(
            src, x_all.at[pos, :, cols(c)], zg_s.at[c, pos], zg_r.at[c, pos],
            up if upward else down, h,
        )

    def gather_start(c):
        gather_copy(c, 1, True, own=True).start()
        gather_copy(c, NZ - 1, False, own=True).start()

    def gather_hop(c, s):
        lu = up_len(c)
        ld = NZ - 1 - lu
        if s <= lu:
            gather_copy(c, s, True, own=s == 1).wait_recv()
            if s < lu:
                gather_copy(c, s + 1, True).start()
        if s <= ld:
            gather_copy(c, NZ - s, False, own=s == 1).wait_recv()
            if s < ld:
                gather_copy(c, NZ - s - 1, False).start()

    def gu_cols(k, half):
        return w_gu.at[:, pl.ds(pl.multiple_of(k * ff + half * ff_half, 128), ff_half)]

    def dn_rows(half):
        return w_dn.at[pl.ds(pl.multiple_of(half * ff_half, 128), ff_half), :]

    def weight_copies():
        mine = [
            pltpu.make_async_copy(w_gate.at[0], gu_cols(0, h), wl.at[0]),
            pltpu.make_async_copy(w_up.at[0], gu_cols(1, h), wl.at[1]),
            pltpu.make_async_copy(w_down.at[0], dn_rows(h), wl.at[2]),
        ]
        sent = [
            remote(w_gate.at[0], gu_cols(0, h), ws.at[0], wr.at[0], ep, 1 - h),
            remote(w_up.at[0], gu_cols(1, h), ws.at[1], wr.at[1], ep, 1 - h),
            remote(w_down.at[0], dn_rows(h), ws.at[2], wr.at[2], ep, 1 - h),
        ]
        return mine, sent

    def build_slots():
        for i in range(1, NZ):
            meta_copy(i).wait_recv()
        ids = jnp.concatenate([meta_all[p, 0:8, :] for p in range(NZ)], axis=1)
        gws = jnp.concatenate([meta_all[p, 8:16, :] for p in range(NZ)], axis=1)
        members, weights = [], []
        for o in range(PLANE):
            ox, oy = o // NY, o % NY
            expert = z * PLANE + lax.rem(x + ox, NX) * NY + lax.rem(y + oy, NY)
            hit = ids == expert.astype(F32)
            members.append(jnp.sum(jnp.where(hit, 1.0, 0.0), axis=0, keepdims=True))
            weights.append(jnp.sum(jnp.where(hit, gws, 0.0), axis=0, keepdims=True))
        member = jnp.concatenate(members, axis=0)
        weight_of[...] = jnp.concatenate(weights, axis=0)
        before = (
            lax.broadcasted_iota(jnp.int32, (tok, tok), 0)
            < lax.broadcasted_iota(jnp.int32, (tok, tok), 1)
        )
        before = jnp.where(before, 1.0, 0.0).astype(BF)
        for p in range(NZ):
            m = member[:, p * tok:(p + 1) * tok]
            rank = jnp.dot(m.astype(BF), before, preferred_element_type=F32)
            slot_of[:, p * tok:(p + 1) * tok] = jnp.where(m > 0.5, rank + float(p * CAP), -1.0)

    def build_pack(first, last):
        r = lax.broadcasted_iota(jnp.int32, (SLOTS, NZ * tok), 0).astype(F32)
        for o in range(first, last):
            here = slot_of[o:o + 1, :] == r
            pack[o * SLOTS:(o + 1) * SLOTS, :] = jnp.where(here, 1.0, 0.0).astype(BF)

    def build_comb(first, last):
        e_row = lax.broadcasted_iota(jnp.int32, (PLANE, 256), 0)
        for q in range(first, last):
            lane = lax.broadcasted_iota(jnp.int32, (PLANE, 256), 1) + q * 256
            low = e_row * SLOTS
            spread = jnp.where((lane >= low) & (lane < low + SLOTS), 1.0, 0.0).astype(BF)
            slots_at = lax.dot_general(
                slot_of[...].astype(BF), spread, (((0,), (0,)), ((), ())),
                preferred_element_type=F32)
            weights_at = lax.dot_general(
                weight_of[...].astype(BF), spread, (((0,), (0,)), ((), ())),
                preferred_element_type=F32)
            r = lax.rem(
                lax.broadcasted_iota(jnp.int32, (1, 256), 1) + q * 256, SLOTS).astype(F32)
            comb[:, q * 256:(q + 1) * 256] = jnp.where(slots_at == r, weights_at, 0.0).astype(BF)

    def dispatch_copy(c, o):
        ox, oy = lax.div(o, NY), lax.rem(o, NY)
        to = z * PLANE + lax.rem(x + ox, NX) * NY + lax.rem(y + oy, NY)
        j = ox * 2 + lax.div(oy, 2)
        return remote(
            packed.at[o, :, cols(c)], rows.at[h, j, :, cols(c)],
            d_s.at[c, o], d_r.at[c, h * 8 + j], to, lax.rem(ox + oy, 2),
        )

    def dispatch(c):
        for g in range(2):
            n = PLANE // 2
            block = jnp.dot(
                pack[g * nrow:(g + 1) * nrow, :],
                x_all[:, :, cols(c)].reshape(NZ * tok, CHUNKS[c][1]),
                preferred_element_type=F32,
            ).astype(BF)
            packed[g * n:(g + 1) * n, :, cols(c)] = block.reshape(n, SLOTS, CHUNKS[c][1])
            start = 1 - h if g == 0 else n

            def send(o, _):
                dispatch_copy(c, o).start()
                return 0

            lax.fori_loop(start, (g + 1) * n, send, 0)
            if g == 0:
                @pl.when(h == 0)
                def _():
                    rows[0, 0, :, cols(c)] = packed[0, :, cols(c)]

    def dispatch_wait(c):
        def wait(i, _):
            remote(
                packed.at[0, :, cols(c)], rows.at[lax.div(i, 8), lax.rem(i, 8), :, cols(c)],
                d_s.at[c, 0], d_r.at[c, i], ep, 1 - h,
            ).wait_recv()
            return 0

        lax.fori_loop(1 - h, PLANE, wait, 0)

    last = len(CHUNKS) - 1

    def expert_in(c):
        start, width = CHUNKS[c]
        if c < last:
            for n in range(0, 2 * ff, 512):
                total = None
                for hs in range(2):
                    left = rows[hs, :, :, cols(c)].reshape(nrow, width)
                    right = w_gu[hs * half_width + start:hs * half_width + start + width, n:n + 512]
                    term = jnp.dot(left, right, preferred_element_type=F32)
                    total = term if total is None else total + term
                acc[:, n:n + 512] = total if c == 0 else acc[:, n:n + 512] + total
        else:
            for n in range(0, ff, 256):
                g, u = acc[:, n:n + 256], acc[:, ff + n:ff + n + 256]
                for hs in range(2):
                    left = rows[hs, :, :, cols(c)].reshape(nrow, width)
                    k = pl.ds(hs * half_width + start, width)
                    g = g + jnp.dot(left, w_gu[k, n:n + 256], preferred_element_type=F32)
                    u = u + jnp.dot(left, w_gu[k, ff + n:ff + n + 256], preferred_element_type=F32)
                hidden[:, n:n + 256] = (g / (1.0 + jnp.exp(-g)) * u).astype(BF)

    def return_copy(c, i):
        hd, j = lax.div(i, 8), lax.rem(i, 8)
        ox = lax.div(j, 2)
        oy = 2 * lax.rem(j, 2) + lax.rem(ox + h, 2)
        to = z * PLANE + lax.rem(x - ox + NX, NX) * NY + lax.rem(y - oy + NY, NY)
        return remote(
            y_out.at[hd, j, :, cols(c)], y_in.at[ox * NY + oy, :, cols(c)],
            b_s.at[c, i], b_r.at[c, ox * NY + oy], to, hd,
        )

    def expert_out(c):
        start, width = CHUNKS[c]
        for hd in range(2):
            block = jnp.dot(
                hidden[...], w_dn[:, hd * half_width + start:hd * half_width + start + width],
                preferred_element_type=F32,
            ).astype(BF)
            y_out[hd, :, :, cols(c)] = block.reshape(PLANE // 2, SLOTS, width)
            start_i = 1 - h if hd == 0 else 8

            def send(i, _):
                return_copy(c, i).start()
                return 0

            lax.fori_loop(start_i, 8 * (hd + 1), send, 0)
            if hd == 0:
                @pl.when(h == 0)
                def _():
                    y_in[0, :, cols(c)] = y_out[0, 0, :, cols(c)]

    def return_wait(c):
        def wait(o, _):
            remote(
                y_out.at[0, 0, :, cols(c)], y_in.at[o, :, cols(c)],
                b_s.at[c, 0], b_r.at[c, o], ep, 1 - h,
            ).wait_recv()
            return 0

        lax.fori_loop(1 - h, PLANE, wait, 0)

    def reduce_copy(c, pos, downward):
        to_pos = pos - 1 if downward else pos + 1
        return remote(
            red_out.at[pos, :, cols(c)], red_in.at[to_pos, :, cols(c)],
            zr_s.at[c, pos], zr_r.at[c, to_pos], down if downward else up, h,
        )

    def combine(c):
        width = CHUNKS[c][1]
        return_wait(c)
        part[:, cols(c)] = jnp.dot(
            comb[...], y_in[:, :, cols(c)].reshape(PLANE * SLOTS, width),
            preferred_element_type=F32)
        a, b = up_len(c), up_len(c) + 1
        for pos, downward in ((a, True), (b, False)):
            red_out[pos, :, cols(c)] = part[pos * tok:(pos + 1) * tok, cols(c)].astype(BF)
            reduce_copy(c, pos, downward).start()

    def reduce_hop(c, s):
        a, b = up_len(c) - (s - 1), up_len(c) + 1 + (s - 1)
        for pos, downward in ((a, True), (b, False)):
            if 1 <= pos <= NZ - 1:
                reduce_copy(c, pos + 1 if downward else pos - 1, downward).wait_recv()
                total = part[pos * tok:(pos + 1) * tok, cols(c)] + red_in[pos, :, cols(c)].astype(F32)
                red_out[pos, :, cols(c)] = total.astype(BF)
                reduce_copy(c, pos, downward).start()

    def finish(c):
        reduce_copy(c, 1, True).wait_recv()
        reduce_copy(c, NZ - 1, False).wait_recv()
        total = part[0:tok, cols(c)] + red_in[0, :, cols(c)].astype(F32)
        total = total + red_in[NZ, :, cols(c)].astype(F32)
        out[:, cols(c)] = total.astype(BF)

    for i in range(1, NZ):
        meta_copy(i).start()
    meta_all[0] = meta[...]
    mine, sent = weight_copies()

    def start_weights():
        for cp in mine:
            cp.start()
        for cp in sent:
            cp.start()

    def wait_weights():
        for cp in mine:
            cp.wait()
        for cp in sent:
            cp.wait_recv()

    events = []
    nc = len(CHUNKS)
    for c in range(nc):
        t0 = 2.0 * c
        events.append((t0, functools.partial(gather_start, c)))
        for s in range(1, 5):
            events.append((t0 + s, functools.partial(gather_hop, c, s)))
        events.append((t0 + 4.3, functools.partial(dispatch, c)))
        events.append((t0 + 7.6, functools.partial(dispatch_wait, c)))
        events.append((t0 + 7.7, functools.partial(expert_in, c)))
    events.append((0.2, start_weights))
    events.append((1.2, build_slots))
    events.append((1.4, functools.partial(build_pack, 0, 4)))
    events.append((2.4, functools.partial(build_pack, 4, 10)))
    events.append((3.4, functools.partial(build_pack, 10, 16)))
    events.append((7.55, wait_weights))
    events.append((10.5, functools.partial(build_comb, 0, 5)))
    x_all[0] = tokens[...]
    for _, event in sorted(events, key=lambda e: e[0]):
        event()
    for c in range(nc):
        expert_out(c)
    events = []
    for c in range(nc):
        t0 = 2.5 * c
        events.append((t0, functools.partial(combine, c)))
        for s in range(2, 5):
            events.append((t0 + s - 1, functools.partial(reduce_hop, c, s)))
        events.append((t0 + 4, functools.partial(finish, c)))
    for _, event in sorted(events, key=lambda e: e[0]):
        event()

    for i in range(1, NZ):
        meta_copy(i).wait_send()
    for cp in sent:
        cp.wait_send()
    for c in range(nc):
        lu = up_len(c)
        for pos in range(1, NZ):
            gather_copy(c, pos, pos <= lu, own=pos in (1, NZ - 1)).wait_send()
            reduce_copy(c, pos, pos <= lu).wait_send()

        def drain(i, _):
            dispatch_copy(c, i).wait_send()
            return_copy(c, i).wait_send()
            return 0

        lax.fori_loop(1 - h, PLANE, drain, 0)


def local(tokens, gate_weights, expert_ids, w_gate, w_up, w_down):
    tok, half_width = tokens.shape
    ff_half = w_gate.shape[2]
    width, ff = 2 * half_width, 2 * ff_half
    nrow = (PLANE // 2) * SLOTS
    nc = len(CHUNKS)
    meta = jnp.concatenate([expert_ids.astype(F32).T, gate_weights.T], axis=0)
    vmem = pl.BlockSpec(memory_space=pltpu.VMEM)
    hbm = pl.BlockSpec(memory_space=pl.ANY)
    dma = pltpu.SemaphoreType.DMA
    return pl.pallas_call(
        kernel,
        name="moe",
        out_shape=jax.ShapeDtypeStruct((tok, half_width), BF),
        in_specs=[vmem, vmem, hbm, hbm, hbm],
        out_specs=vmem,
        scratch_shapes=[
            pltpu.VMEM((NZ, tok, half_width), BF),
            pltpu.VMEM((NZ, 16, tok), F32),
            pltpu.VMEM((PLANE, NZ * tok), F32),
            pltpu.VMEM((PLANE, NZ * tok), F32),
            pltpu.VMEM((PLANE * SLOTS, NZ * tok), BF),
            pltpu.VMEM((NZ * tok, PLANE * SLOTS), BF),
            pltpu.VMEM((PLANE, SLOTS, half_width), BF),
            pltpu.VMEM((2, PLANE // 2, SLOTS, half_width), BF),
            pltpu.VMEM((width, 2 * ff), BF),
            pltpu.VMEM((ff, width), BF),
            pltpu.VMEM((nrow, 2 * ff), F32),
            pltpu.VMEM((nrow, ff), BF),
            pltpu.VMEM((2, PLANE // 2, SLOTS, half_width), BF),
            pltpu.VMEM((PLANE, SLOTS, half_width), BF),
            pltpu.VMEM((NZ * tok, half_width), F32),
            pltpu.VMEM((NZ, tok, half_width), BF),
            pltpu.VMEM((NZ + 1, tok, half_width), BF),
            dma((NZ,)), dma((NZ,)),
            dma((nc, NZ)), dma((nc, NZ)),
            dma((nc, PLANE)), dma((nc, PLANE)),
            dma((nc, PLANE)), dma((nc, PLANE)),
            dma((nc, NZ)), dma((nc, NZ + 1)),
            dma((3,)), dma((3,)), dma((3,)),
        ],
        compiler_params=pltpu.CompilerParams(
            collective_id=0, has_side_effects=True, vmem_limit_bytes=60 * 2**20
        ),
    )(tokens, meta, w_gate, w_up, w_down)


def solution(mesh):
    placed = (
        P("ep", "half"),
        P("ep", None),
        P("ep", None),
        P("ep", None, "half"),
        P("ep", None, "half"),
        P("ep", "half", None),
    )
    return jax.shard_map(
        local, mesh=mesh, in_specs=placed, out_specs=P("ep", "half"), check_vma=False
    )
```

time: 342 us -> 126 us (0.37)
  Pallas kernels: 0 us -> 120 us
  blocking collectives: 120 us -> 0 us
  waiting for transfers between devices: 113 us -> 0 us
  local copies, waits for them, and re-layouts: 51.4 us -> 1.67 us
  matrix products: 19.2 us -> 0 us
  starting transfers between devices: 14.3 us -> 0 us
  between operations: 13.5 us -> 0.01 us
  other arithmetic: 10.1 us -> 1.97 us
    pallas_call x0 -> x1, Pallas kernels: none -> 120 us  [local(): pl.pallas_call(kernel, name='moe', out_shape=jax.ShapeDtypeStruct((tok, h...]
    all_to_all x2 -> x0, blocking collectives: 120 us -> none  [the longest x1 111 us: local(): lax.all_to_all(outgoing, 'ep', split_axis=0, concat_axis=0, tiled=True)]
    all_to_all x1 -> x0, waiting for transfers between devices: 95.5 us -> none  [local(): lax.all_to_all(summed, 'ep', split_axis=0, concat_axis=0, tiled=True)]
    dot_general x3 -> x0, matrix products: 19.2 us -> none  [the longest x1 9.81 us: local(): jnp.einsum('secf,efd->secd', hidden, w_down, preferred_element_type=jnp.f...]
    gather x3 -> x0, local copies, waits for them, and re-layouts: 19.1 us -> none  [the longest x2 11 us: local(): tokens[token_table] * filled[:, None]]
    all_gather x1 -> x0, waiting for transfers between devices: 17.5 us -> none  [local(): whole = lax.all_gather(received, 'half', axis=2, tiled=True)]
    all_to_all x1 -> x0, starting transfers between devices: 14.3 us -> none  [local(): lax.all_to_all(summed, 'ep', split_axis=0, concat_axis=0, tiled=True)]
    scatter x2 -> x0, local copies, waits for them, and re-layouts: 11.9 us -> none  [the longest x1 7.58 us: local(): filled = jnp.zeros((experts * capacity,), jnp.bfloat16).at[slot].set(jnp....]
  transfers between devices with their start and end apart: 2 -> 0, of which waited for: 2 -> 0; matrix products, arithmetic and copies ran while one was open for 0% -> 0% of each run, Pallas kernels for 0% -> 0%
where the time goes in v1:
time: 126 us; the launch traced here: 124 us
  Pallas kernels  120 us (95%)
  other arithmetic  1.97 us (2%)
  local copies, waits for them, and re-layouts  1.67 us (1%)
    pallas_call x1, Pallas kernels, local(): pl.pallas_call(kernel, name='moe', out_shape=jax.ShapeDtypeStruct((tok, h...  120 us

profile of v1, /device:TPU:8, one launch (start us, length us, event | category | flops | bytes accessed | tf_op | source)
XLA Modules:
  0.0 124.0 jit_solution(7630523900479236771)
XLA Ops:
  0.0 0.7 convert_bitcast_fusion
  0.7 1.3 %pad_maximum_fusion.meta = f32[16,128]{1,0:T(8,128)} fusion(f32[8,128]{1,0:T(8,128)} %bitcast.3, f32[8,128]{1,0:T(8,128)S(1)} %convert_bitcast_fusion), kind=kLoop, calls=%fused_computation | loop fusion | flops 2048 | bytes 16384 | tf_op jit(solution)/shard_map/concatenate | solution.py:378
  2.0 120.3 %moe.1 = bf16[128,1024]{1,0:T(8,128)(2,1)} custom-call(bf16[128,1024]{1,0:T(8,128)(2,1)} %tokens.1, f32[16,128]{1,0:T(8,128)} %pad_maximum_fusion.meta, bf16[1,2048,384]{2,1,0:T(8,128)(2,1)} %w_gate.1, bf16[1,2048,384]{2,1,0:T(8,128)(2,1)} %w_up.1, bf16[1,384,2048]{2,1,0:T(8,128)(2,1)} %w_down.1), custom_call_target="tpu_custom_call" | custom-call | tf_op jit(solution)/shard_map/moe/pallas_call | solution.py:382
  122.3 1.7 %copy.8 = bf16[128,1024]{1,0:T(8,128)(2,1)} copy(bf16[128,1024]{1,0:T(8,128)(2,1)} %moe.1) | data formatting | bytes 524288
